TPU v7x, 32 devices: a whole 2x2x4 slice. The times are simulated.
32 devices in a mesh: dp: 8 (over z, y), mp: 4 (over x, core).
Axes of the slice: x: 2, y: 2, z: 4, core: 2. Of those that a mesh axis runs over, the one named last changes fastest.
Arguments:
- queries: bfloat16 [4096, 4096], P('dp', 'mp'), may hold values from -6 to 6
- passages: bfloat16 [4096, 4096], P('dp', 'mp'), may hold values from -6 to 6
- labels: int32 [4096], P('dp'), may hold values from 0 to 4095
- projection: bfloat16 [4096, 128], P('mp'), may hold values from -0.09375 to 0.09375
Outputs:
- loss: float32 [4096], P('dp')
- query_embed: bfloat16 [4096, 128], P('dp')
All inputs are finite; a program needn't handle non-finite values.
Results may differ from a plain program's by a relative error of at most 0.0039.
Values may be sent and summed in bfloat16 or wider, within the bound.
No kernel may reach another device: no remote copies, remote signals or barrier semaphores. Data moves between devices by JAX's collectives and lax.ppermute only.
A program may use at most 64 MiB of HBM per device.

v0:
```python
import jax
import jax.numpy as jnp
from jax import lax
from jax.sharding import PartitionSpec as P


def merged(part, axis, combine):
    gathered = jax.tree.map(lambda a: lax.all_gather(a, axis), part)

    def take(source):
        return jax.tree.map(lambda a: lax.dynamic_index_in_dim(a, source, 0, False), gathered)

    return lax.fori_loop(
        1, lax.axis_size(axis), lambda source, state: combine(state, take(source)), take(0)
    )


def combine_stats(first, second):
    top = jnp.maximum(first[0], second[0])
    total = first[1] * jnp.exp(first[0] - top) + second[1] * jnp.exp(second[0] - top)
    return (top, total, first[2] + second[2])


def block_columns(count):
    target = 2048
    if count <= target:
        return count
    best = 1
    for option in range(1, target + 1):
        if count % option == 0:
            best = option
    return best


def per_device(queries, passages, labels, projection):
    query_part = jnp.dot(queries, projection, preferred_element_type=jnp.float32)
    passage_part = jnp.dot(passages, projection, preferred_element_type=jnp.float32)
    rows = query_part.shape[0]
    embed = query_part.shape[1]
    query_embed = lax.psum(query_part, "mp").astype(jnp.bfloat16)
    passage_embed = lax.psum_scatter(
        passage_part.astype(jnp.bfloat16), "mp", scatter_dimension=0, tiled=True
    )
    offset = lax.axis_index("mp") * passage_embed.shape[0]
    width = passage_embed.shape[0]
    start_state = (
        jnp.full((rows,), -jnp.inf, jnp.float32),
        jnp.zeros((rows,), jnp.float32),
        jnp.zeros((rows,), jnp.float32),
    )
    piece = lax.all_gather(passage_embed, "dp", axis=0, tiled=True)
    count = piece.shape[0]
    columns_each = block_columns(count)
    blocks = piece.reshape(count // columns_each, columns_each, embed)
    firsts = jnp.arange(blocks.shape[0], dtype=jnp.int32) * columns_each

    def step(state, item):
        block, first = item
        scores = lax.dot_general(
            query_embed, block, (((1,), (1,)), ((), ())), preferred_element_type=jnp.float32
        )
        columns = first + lax.iota(jnp.int32, columns_each)
        passage_ids = columns // width * rows + offset + columns % width
        hit = passage_ids[None, :] == labels[:, None]
        chosen = jnp.sum(jnp.where(hit, scores, 0.0), axis=1)
        block_top = jnp.max(scores, axis=1)
        block_sum = jnp.sum(jnp.exp(scores - block_top[:, None]), axis=1)
        return (combine_stats(state, (block_top, block_sum, chosen)), None)

    result, unused = lax.scan(step, start_state, (blocks, firsts))
    top, total, chosen = merged(result, "mp", combine_stats)
    loss = top + jnp.log(total) - chosen
    return (loss, query_embed)


def solution(mesh):
    return jax.shard_map(
        per_device,
        mesh=mesh,
        in_specs=(P("dp", "mp"), P("dp", "mp"), P("dp"), P("mp", None)),
        out_specs=(P("dp"), P("dp", None)),
        check_vma=False,
    )
```

profile of v0, /device:TPU:0, one launch (start us, length us, event | category | flops | bytes accessed | tf_op | source)
XLA Modules:
  0.0 88.4 jit_solution(6473758463576834238)
XLA Ops:
  7.2 0.0 copy-start
  7.2 0.0 reduce-scatter.2.cloned.1.call-start
  7.2 1.2 %copy-done = bf16[512,1024]{1,0:T(8,128)(2,1)S(1)} copy-done((bf16[512,1024]{1,0:T(8,128)(2,1)S(1)}, bf16[512,1024]{1,0:T(8,128)(2,1)}, u32[]{:S(2)}) %copy-start) | copy-done | bytes 1048600
  8.4 2.0 %convolution_convert_fusion = bf16[512,128]{1,0:T(8,128)(2,1)} fusion(bf16[512,1024]{1,0:T(8,128)(2,1)S(1)} %copy-done, bf16[1024,128]{1,0:T(8,128)(2,1)} %param.9), kind=kOutput, calls=%fused_computation.6 | convolution fusion | flops 134283264 | bytes 1441792 | tf_op jit(solution)/shard_map/dot_general | solution.py:37
  10.4 0.0 reduce-scatter.2.cloned.1.call-update
  10.4 0.0 copy-start.2
  10.5 1.7 %fusion.11 = f32[512,128]{1,0:T(8,128)S(1)} fusion(bf16[512,1024]{1,0:T(8,128)(2,1)} %param.6, bf16[1024,128]{1,0:T(8,128)(2,1)} %param.9), kind=kOutput, calls=%fused_computation.27 | convolution fusion | flops 134217728 | bytes 1572864 | tf_op jit(solution)/shard_map/dot_general | solution.py:36
  12.2 16.3 %all-reduce.1 = bf16[512,128]{1,0:T(8,128)(2,1)S(1)} all-reduce(f32[512,128]{1,0:T(8,128)S(1)} %fusion.11), channel_id=1, replica_groups=mesh['dp'=8,'mp'=4] {'mp'}, use_global_device_ids=true, to_apply=%region_0.0 | all-reduce | flops 65536 | bytes 393216 | tf_op jit(solution)/shard_map/psum | solution.py:40
  28.5 0.0 copy-start.1
  28.5 4.5 %reduce-scatter.2.cloned.1.call-done = bf16[128,128]{1,0:T(8,128)(2,1)} async-done(((bf16[512,128]{1,0:T(8,128)(2,1)}), bf16[128,128]{1,0:T(8,128)(2,1)}) %reduce-scatter.2.cloned.1.call-update) | async-done | bytes 32784 | tf_op jit(solution)/shard_map/reduce_scatter | solution.py:41
  33.0 31.0 %all_gather.19 = bf16[1024,128]{1,0:T(8,128)(2,1)S(1)} all-gather(bf16[128,128]{1,0:T(8,128)(2,1)} %reduce-scatter.2.cloned.1.call-done), channel_id=1, replica_groups=mesh['dp'=8,'mp'=4] {'dp'}, dimensions={0}, use_global_device_ids=true | all-gather | bytes 294912 | tf_op jit(solution)/shard_map/all_gather | solution.py:51
  64.0 0.5 fusion.10
  64.5 0.0 copy-done.2
  64.5 0.7 select_reduce_fusion
  65.2 0.0 copy-done.1
  65.2 5.2 %all-gather.3 = f32[4,1,512]{2,1,0:T(1,128)S(1)} all-gather(f32[1,1,512]{2,1,0:T(1,128)S(1)} %bitcast.40), channel_id=1, replica_groups=mesh['dp'=8,'mp'=4] {'mp'}, dimensions={0}, use_global_device_ids=true | all-gather | bytes 10240 | tf_op jit(solution)/shard_map/all_gather | solution.py:8
  70.4 5.2 %all-gather.4 = f32[4,1,512]{2,1,0:T(1,128)S(1)} all-gather(f32[1,1,512]{2,1,0:T(1,128)S(1)} %bitcast.41), channel_id=3, replica_groups=mesh['dp'=8,'mp'=4] {'mp'}, dimensions={0}, use_global_device_ids=true | all-gather | bytes 10240 | tf_op jit(solution)/shard_map/all_gather | solution.py:8
  75.6 5.2 %all-gather.2 = f32[4,1,512]{2,1,0:T(1,128)S(1)} all-gather(f32[1,1,512]{2,1,0:T(1,128)S(1)} %bitcast.39), channel_id=2, replica_groups=mesh['dp'=8,'mp'=4] {'mp'}, dimensions={0}, use_global_device_ids=true | all-gather | bytes 10240 | tf_op jit(solution)/shard_map/all_gather | solution.py:8
  80.7 0.2 while.12
  81.0 0.6 add_subtract_fusion
  (20 shorter events, 0.2 us)
Async XLA Ops:
  7.2 1.2 %copy-start = (bf16[512,1024]{1,0:T(8,128)(2,1)S(1)}, bf16[512,1024]{1,0:T(8,128)(2,1)}, u32[]{:S(2)}) copy-start(bf16[512,1024]{1,0:T(8,128)(2,1)} %param.7) | copy-start | bytes 3145732
  7.2 25.8 %reduce-scatter.2.cloned.1.call-start = ((), (), s32[]{:S(2)}) async-start(), calls=%async_computation.1 | async-start | bytes 163840 | tf_op jit(solution)/shard_map/reduce_scatter | solution.py:41
  10.4 54.0 %copy-start.2 = (s32[512]{0:T(512)S(1)}, s32[512]{0:T(512)}, u32[]{:S(2)}) copy-start(s32[512]{0:T(512)} %param.8) | copy-start | bytes 6148
  28.5 36.7 %copy-start.1 = (bf16[512,128]{1,0:T(8,128)(2,1)}, bf16[512,128]{1,0:T(8,128)(2,1)S(1)}, u32[]{:S(2)}) copy-start(bf16[512,128]{1,0:T(8,128)(2,1)S(1)} %all-reduce.1) | copy-start | bytes 393220
Sparse Core Ops, SparseCore 0:
  10.6 22.3 reduce-scatter.1
where the time goes:
time: 88.7 us; the launch traced here: 88.4 us
  blocking collectives  62.8 us (71%)
  between operations  14.1 us (16%)
  waiting for transfers between devices  4.51 us (5%)
  matrix products  4.24 us (5%)
  other arithmetic  1.37 us (2%)
  local copies, waits for them, and re-layouts  1.26 us (1%)
    all_gather x1, blocking collectives, per_device(): piece = lax.all_gather(passage_embed, 'dp', axis=0, tiled=True)  31 us
    psum x1, blocking collectives, per_device(): query_embed = lax.psum(query_part, 'mp').astype(jnp.bfloat16)  16.3 us
    all_gather x3, blocking collectives, merged(): gathered = jax.tree.map(lambda a: lax.all_gather(a, axis), part)  15.5 us
    reduce_scatter x1, waiting for transfers between devices, per_device(): lax.psum_scatter(passage_part.astype(jnp.bfloat16), 'mp', scatter_dimensi...  4.5 us
    dot_general x1, matrix products, per_device(): jnp.dot(passages, projection, preferred_element_type=jnp.float32)  2.03 us
  transfers between devices with their start and end apart: 1, of which 1 were waited for; matrix products, arithmetic and copies ran while one was open for 2% of the time, Pallas kernels for 0%

commit v1 on v0

--- a/solution.py
+++ b/solution.py
@@ -48,7 +48,12 @@
         jnp.zeros((rows,), jnp.float32),
         jnp.zeros((rows,), jnp.float32),
     )
-    piece = lax.all_gather(passage_embed, "dp", axis=0, tiled=True)
+    ring = [passage_embed]
+    for hop in range(7):
+        ring.append(lax.ppermute(ring[-1], "dp", [(dev, (dev + 1) % 8) for dev in range(8)]))
+    piece = jnp.roll(
+        jnp.concatenate(ring[::-1], axis=0), (lax.axis_index("dp") + 1) * ring[0].shape[0], axis=0
+    )
     count = piece.shape[0]
     columns_each = block_columns(count)
     blocks = piece.reshape(count // columns_each, columns_each, embed)

time: 88.7 us -> 112 us (1.26)
  waiting for transfers between devices: 4.51 us -> 59.6 us
  blocking collectives: 62.8 us -> 29.2 us
  starting transfers between devices: 0.04 us -> 1.57 us
    ppermute x0 -> x7, waiting for transfers between devices: none -> 36.7 us  [per_device(): lax.ppermute(ring[-1], 'dp', [(dev, (dev + 1) % 8) for dev in range(8)])]
    all_gather x1 -> x0, blocking collectives: 31 us -> none  [per_device(): piece = lax.all_gather(passage_embed, 'dp', axis=0, tiled=True)]
    reduce_scatter x1, waiting for transfers between devices: 4.5 us -> 22.9 us  [per_device(): lax.psum_scatter(passage_part.astype(jnp.bfloat16), 'mp', scatter_dimensi...]
    psum x1, blocking collectives: 16.3 us -> 13.7 us  [per_device(): query_embed = lax.psum(query_part, 'mp').astype(jnp.bfloat16)]
    ppermute x0 -> x7, starting transfers between devices: none -> 1.53 us  [per_device(): lax.ppermute(ring[-1], 'dp', [(dev, (dev + 1) % 8) for dev in range(8)])]
  transfers between devices with their start and end apart: 1 -> 8, of which waited for: 1 -> 7; matrix products, arithmetic and copies ran while one was open for 2% -> 2% of each run, Pallas kernels for 0% -> 0%
where the time goes in v1:
time: 112 us
  waiting for transfers between devices  59.6 us (53%)
  blocking collectives  29.2 us (26%)
  between operations  14.2 us (13%)
  matrix products  4.27 us (4%)
  starting transfers between devices  1.57 us (1%)
  local copies, waits for them, and re-layouts  1.43 us (1%)
  other arithmetic  1.37 us (1%)
    ppermute x7, waiting for transfers between devices, per_device(): lax.ppermute(ring[-1], 'dp', [(dev, (dev + 1) % 8) for dev in range(8)])  36.7 us
    reduce_scatter x1, waiting for transfers between devices, per_device(): lax.psum_scatter(passage_part.astype(jnp.bfloat16), 'mp', scatter_dimensi...  22.9 us
    all_gather x3, blocking collectives, merged(): gathered = jax.tree.map(lambda a: lax.all_gather(a, axis), part)  15.5 us
    psum x1, blocking collectives, per_device(): query_embed = lax.psum(query_part, 'mp').astype(jnp.bfloat16)  13.7 us
  transfers between devices with their start and end apart: 8, of which 7 were waited for; matrix products, arithmetic and copies ran while one was open for 2% of the time, Pallas kernels for 0%

profile of v1, /device:TPU:0, one launch (start us, length us, event | category | flops | bytes accessed | tf_op | source)
XLA Modules:
  0.0 111.8 jit_solution(1221890776886086560)
XLA Ops:
  7.2 0.0 copy-start
  7.2 0.0 reduce-scatter.2.cloned.1.call-start
  7.2 1.2 %copy-done = bf16[512,1024]{1,0:T(8,128)(2,1)S(1)} copy-done((bf16[512,1024]{1,0:T(8,128)(2,1)S(1)}, bf16[512,1024]{1,0:T(8,128)(2,1)}, u32[]{:S(2)}) %copy-start) | copy-done | bytes 1048600
  8.4 2.0 %convolution_convert_fusion = bf16[512,128]{1,0:T(8,128)(2,1)} fusion(bf16[512,1024]{1,0:T(8,128)(2,1)S(1)} %copy-done, bf16[1024,128]{1,0:T(8,128)(2,1)} %param.9), kind=kOutput, calls=%fused_computation.6 | convolution fusion | flops 134283264 | bytes 1441792 | tf_op jit(solution)/shard_map/dot_general | solution.py:37
  10.4 0.0 reduce-scatter.2.cloned.1.call-update
  10.5 22.9 %reduce-scatter.2.cloned.1.call-done = bf16[128,128]{1,0:T(8,128)(2,1)} async-done(((bf16[512,128]{1,0:T(8,128)(2,1)}), bf16[128,128]{1,0:T(8,128)(2,1)}) %reduce-scatter.2.cloned.1.call-update) | async-done | bytes 32784 | tf_op jit(solution)/shard_map/reduce_scatter | solution.py:41
  33.4 1.5 %collective-permute-start = (bf16[128,128]{1,0:T(8,128)(2,1)}, bf16[128,128]{1,0:T(8,128)(2,1)S(1)}, u32[]{:S(2)}, u32[]{:S(2)}) collective-permute-start(bf16[128,128]{1,0:T(8,128)(2,1)} %reduce-scatter.2.cloned.1.call-done), channel_id=1, source_target_pairs={{0,4},{4,8},{8,12},{12,16},{16,20},{20,24},{24,28},{28,0},{1,5},{5... | collective-permute-start | bytes 98312 | tf_op jit(solution)/shard_map/ppermute | solution.py:53
  34.8 5.4 %collective-permute-done = bf16[128,128]{1,0:T(8,128)(2,1)S(1)} collective-permute-done((bf16[128,128]{1,0:T(8,128)(2,1)}, bf16[128,128]{1,0:T(8,128)(2,1)S(1)}, u32[]{:S(2)}, u32[]{:S(2)}) %collective-permute-start) | collective-permute-done | bytes 32800 | tf_op jit(solution)/shard_map/ppermute | solution.py:53
  40.2 0.0 collective-permute-start.1
  40.2 6.6 %collective-permute-done.1 = bf16[128,128]{1,0:T(8,128)(2,1)S(1)} collective-permute-done((bf16[128,128]{1,0:T(8,128)(2,1)S(1)}, bf16[128,128]{1,0:T(8,128)(2,1)S(1)}, u32[]{:S(2)}, u32[]{:S(2)}) %collective-permute-start.1) | collective-permute-done | bytes 32800 | tf_op jit(solution)/shard_map/ppermute | solution.py:53
  46.8 0.0 collective-permute-start.2
  46.8 6.6 %collective-permute-done.2 = bf16[128,128]{1,0:T(8,128)(2,1)S(1)} collective-permute-done((bf16[128,128]{1,0:T(8,128)(2,1)S(1)}, bf16[128,128]{1,0:T(8,128)(2,1)S(1)}, u32[]{:S(2)}, u32[]{:S(2)}) %collective-permute-start.2) | collective-permute-done | bytes 32800 | tf_op jit(solution)/shard_map/ppermute | solution.py:53
  53.4 0.0 collective-permute-start.3
  53.4 6.6 %collective-permute-done.3 = bf16[128,128]{1,0:T(8,128)(2,1)S(1)} collective-permute-done((bf16[128,128]{1,0:T(8,128)(2,1)S(1)}, bf16[128,128]{1,0:T(8,128)(2,1)S(1)}, u32[]{:S(2)}, u32[]{:S(2)}) %collective-permute-start.3) | collective-permute-done | bytes 32800 | tf_op jit(solution)/shard_map/ppermute | solution.py:53
  60.1 0.0 collective-permute-start.4
  60.1 1.7 %fusion.14 = f32[512,128]{1,0:T(8,128)S(1)} fusion(bf16[512,1024]{1,0:T(8,128)(2,1)} %param.6, bf16[1024,128]{1,0:T(8,128)(2,1)} %param.9), kind=kOutput, calls=%fused_computation.46 | convolution fusion | flops 134217728 | bytes 1572864 | tf_op jit(solution)/shard_map/dot_general | solution.py:36
  61.8 0.0 copy-start.3
  61.8 4.9 %collective-permute-done.4 = bf16[128,128]{1,0:T(8,128)(2,1)S(1)} collective-permute-done((bf16[128,128]{1,0:T(8,128)(2,1)S(1)}, bf16[128,128]{1,0:T(8,128)(2,1)S(1)}, u32[]{:S(2)}, u32[]{:S(2)}) %collective-permute-start.4) | collective-permute-done | bytes 32800 | tf_op jit(solution)/shard_map/ppermute | solution.py:53
  66.7 0.0 collective-permute-start.5
  66.7 13.7 %all-reduce.1 = bf16[512,128]{1,0:T(8,128)(2,1)S(1)} all-reduce(f32[512,128]{1,0:T(8,128)S(1)} %fusion.14), channel_id=1, replica_groups=mesh['dp'=8,'mp'=4] {'mp'}, use_global_device_ids=true, to_apply=%region_0.0 | all-reduce | flops 65536 | bytes 393216 | tf_op jit(solution)/shard_map/psum | solution.py:40
  80.4 0.0 copy-start.1
  80.4 0.0 collective-permute-done.5
  80.4 0.1 collective-permute-start.6
  80.5 6.6 %collective-permute-done.6 = bf16[128,128]{1,0:T(8,128)(2,1)S(1)} collective-permute-done((bf16[128,128]{1,0:T(8,128)(2,1)S(1)}, bf16[128,128]{1,0:T(8,128)(2,1)S(1)}, u32[]{:S(2)}, u32[]{:S(2)}) %collective-permute-start.6) | collective-permute-done | bytes 32800 | tf_op jit(solution)/shard_map/ppermute | solution.py:53
  87.3 0.5 fusion.13
  87.8 0.7 select_reduce_fusion
  88.5 0.0 copy-done.1
  88.5 5.2 %all-gather.3 = f32[4,1,512]{2,1,0:T(1,128)S(1)} all-gather(f32[1,1,512]{2,1,0:T(1,128)S(1)} %bitcast.39), channel_id=1, replica_groups=mesh['dp'=8,'mp'=4] {'mp'}, dimensions={0}, use_global_device_ids=true | all-gather | bytes 10240 | tf_op jit(solution)/shard_map/all_gather | solution.py:8
  93.7 5.2 %all-gather.4 = f32[4,1,512]{2,1,0:T(1,128)S(1)} all-gather(f32[1,1,512]{2,1,0:T(1,128)S(1)} %bitcast.40), channel_id=3, replica_groups=mesh['dp'=8,'mp'=4] {'mp'}, dimensions={0}, use_global_device_ids=true | all-gather | bytes 10240 | tf_op jit(solution)/shard_map/all_gather | solution.py:8
  98.9 5.2 %all-gather.2 = f32[4,1,512]{2,1,0:T(1,128)S(1)} all-gather(f32[1,1,512]{2,1,0:T(1,128)S(1)} %bitcast.38), channel_id=2, replica_groups=mesh['dp'=8,'mp'=4] {'mp'}, dimensions={0}, use_global_device_ids=true | all-gather | bytes 10240 | tf_op jit(solution)/shard_map/all_gather | solution.py:8
  104.1 0.2 while.12
  104.4 0.6 add_subtract_fusion
  (39 shorter events, 0.3 us)
Async XLA Ops:
  7.2 1.2 %copy-start = (bf16[512,1024]{1,0:T(8,128)(2,1)S(1)}, bf16[512,1024]{1,0:T(8,128)(2,1)}, u32[]{:S(2)}) copy-start(bf16[512,1024]{1,0:T(8,128)(2,1)} %param.7) | copy-start | bytes 3145732
  7.2 26.2 %reduce-scatter.2.cloned.1.call-start = ((), (), s32[]{:S(2)}) async-start(), calls=%async_computation.1 | async-start | bytes 163840 | tf_op jit(solution)/shard_map/reduce_scatter | solution.py:41
  33.4 53.8 %copy-start.2 = (bf16[128,128]{1,0:T(8,128)(2,1)S(1)}, bf16[128,128]{1,0:T(8,128)(2,1)}, u32[]{:S(2)}) copy-start(bf16[128,128]{1,0:T(8,128)(2,1)} %reduce-scatter.2.cloned.1.call-done) | copy-start | bytes 98308
  33.4 6.8 %collective-permute-start = (bf16[128,128]{1,0:T(8,128)(2,1)}, bf16[128,128]{1,0:T(8,128)(2,1)S(1)}, u32[]{:S(2)}, u32[]{:S(2)}) collective-permute-start(bf16[128,128]{1,0:T(8,128)(2,1)} %reduce-scatter.2.cloned.1.call-done), channel_id=1, source_target_pairs={{0,4},{4,8},{8,12},{12,16},{16,20},{20,24},{24,28},{28,0},{1,5},{5... | collective-permute-start | bytes 98312 | tf_op jit(solution)/shard_map/ppermute | solution.py:53
  40.2 6.6 %collective-permute-start.1 = (bf16[128,128]{1,0:T(8,128)(2,1)S(1)}, bf16[128,128]{1,0:T(8,128)(2,1)S(1)}, u32[]{:S(2)}, u32[]{:S(2)}) collective-permute-start(bf16[128,128]{1,0:T(8,128)(2,1)S(1)} %collective-permute-done), channel_id=1, source_target_pairs={{0,4},{4,8},{8,12},{12,16},{16,20},{20,24},{24,28},{28,0},{1,5},{5... | collective-permute-start | bytes 98312 | tf_op jit(solution)/shard_map/ppermute | solution.py:53
  46.8 6.6 %collective-permute-start.2 = (bf16[128,128]{1,0:T(8,128)(2,1)S(1)}, bf16[128,128]{1,0:T(8,128)(2,1)S(1)}, u32[]{:S(2)}, u32[]{:S(2)}) collective-permute-start(bf16[128,128]{1,0:T(8,128)(2,1)S(1)} %collective-permute-done.1), channel_id=1, source_target_pairs={{0,4},{4,8},{8,12},{12,16},{16,20},{20,24},{24,28},{28,0},{1,5},{5... | collective-permute-start | bytes 98312 | tf_op jit(solution)/shard_map/ppermute | solution.py:53
  53.4 6.6 %collective-permute-start.3 = (bf16[128,128]{1,0:T(8,128)(2,1)S(1)}, bf16[128,128]{1,0:T(8,128)(2,1)S(1)}, u32[]{:S(2)}, u32[]{:S(2)}) collective-permute-start(bf16[128,128]{1,0:T(8,128)(2,1)S(1)} %collective-permute-done.2), channel_id=1, source_target_pairs={{0,4},{4,8},{8,12},{12,16},{16,20},{20,24},{24,28},{28,0},{1,5},{5... | collective-permute-start | bytes 98312 | tf_op jit(solution)/shard_map/ppermute | solution.py:53
  60.1 6.6 %collective-permute-start.4 = (bf16[128,128]{1,0:T(8,128)(2,1)S(1)}, bf16[128,128]{1,0:T(8,128)(2,1)S(1)}, u32[]{:S(2)}, u32[]{:S(2)}) collective-permute-start(bf16[128,128]{1,0:T(8,128)(2,1)S(1)} %collective-permute-done.3), channel_id=1, source_target_pairs={{0,4},{4,8},{8,12},{12,16},{16,20},{20,24},{24,28},{28,0},{1,5},{5... | collective-permute-start | bytes 98312 | tf_op jit(solution)/shard_map/ppermute | solution.py:53
  61.8 26.1 %copy-start.3 = (s32[512]{0:T(512)S(1)}, s32[512]{0:T(512)}, u32[]{:S(2)}) copy-start(s32[512]{0:T(512)} %param.8) | copy-start | bytes 6148
  66.7 13.7 %collective-permute-start.5 = (bf16[128,128]{1,0:T(8,128)(2,1)S(1)}, bf16[128,128]{1,0:T(8,128)(2,1)S(1)}, u32[]{:S(2)}, u32[]{:S(2)}) collective-permute-start(bf16[128,128]{1,0:T(8,128)(2,1)S(1)} %collective-permute-done.4), channel_id=1, source_target_pairs={{0,4},{4,8},{8,12},{12,16},{16,20},{20,24},{24,28},{28,0},{1,5},{5... | collective-permute-start | bytes 98312 | tf_op jit(solution)/shard_map/ppermute | solution.py:53
  80.4 8.1 %copy-start.1 = (bf16[512,128]{1,0:T(8,128)(2,1)}, bf16[512,128]{1,0:T(8,128)(2,1)S(1)}, u32[]{:S(2)}) copy-start(bf16[512,128]{1,0:T(8,128)(2,1)S(1)} %all-reduce.1) | copy-start | bytes 393220
  80.4 6.7 %collective-permute-start.6 = (bf16[128,128]{1,0:T(8,128)(2,1)S(1)}, bf16[128,128]{1,0:T(8,128)(2,1)S(1)}, u32[]{:S(2)}, u32[]{:S(2)}) collective-permute-start(bf16[128,128]{1,0:T(8,128)(2,1)S(1)} %collective-permute-done.5), channel_id=1, source_target_pairs={{0,4},{4,8},{8,12},{12,16},{16,20},{20,24},{24,28},{28,0},{1,5},{5... | collective-permute-start | bytes 98312 | tf_op jit(solution)/shard_map/ppermute | solution.py:53
Sparse Core Ops, SparseCore 0:
  11.0 22.3 reduce-scatter.1
